TPU v7x, 32 devices: a whole 2x2x4 slice. The times are simulated.
32 devices in a mesh: gy: 16 (over z, y, core), gz: 2 (over x).
Axes of the slice: x: 2, y: 2, z: 4, core: 2. Of those that a mesh axis runs over, the one named last changes fastest.
Arguments:
- omega: float32 [3, 256, 128, 128], P(None, 'gy', 'gz'), may hold values from -6 to 6
- velocity: float32 [3, 256, 128, 128], P(None, 'gy', 'gz'), may hold values from -6 to 6
- point_owner: int32 [1152], replicated, may hold values from 0 to 22, as said below
- point_cells: int32 [3, 1152], replicated, may hold values from 1 to 125, as said below
- point_frac: float32 [3, 1152], replicated, may hold values from 0 to 1
- chord: float32 [1152], replicated, may hold values from 0.2 to 1
- twist: float32 [1152], replicated, may hold values from -0.3 to 0.3
- angle_step: int32 [1], replicated, may hold values from 0 to 719
Outputs:
- omega_out: float32 [3, 256, 128, 128], P(None, 'gy', 'gz')
- blade_sources: float32 [3, 1152], replicated
Inputs may be any that keep to these rules, and one draw needn't show every extreme that they name: `point_owner`: turbine t's points lie in spanwise blocks t * 2 to (t + 1) * 2 - 1 and in the 1 vertical blocks from (1) // 2 on; no block holds more than 192 points, and in every turbine one block holds exactly 192. `point_cells`: streamwise cells lie in 1 to 125, spanwise in 1 to 13, vertical in 1 to 61; all points of a turbine share one streamwise cell.
All inputs are finite; a program needn't handle non-finite values.
Results may differ from a plain program's by a relative error of at most 0.0003.
Values sent between devices are 32-bit elements; how exact they have to be, the bound alone decides.
A program may use at most 128 MiB of HBM per device.

v0:
```python
import jax
import jax.numpy as jnp
from jax import lax
from jax.sharding import PartitionSpec as P

TURBINES = 6
BLADES = 3
BP = 64


section_step = 0.4
viscosity = 0.05
tip_speed = 3.0
turn_step = 2.0 * 3.141592653589793 / 720.0


def with_halo(x, sides, width):
    for axis, dim in sides:
        size, length = (lax.axis_size(axis), x.shape[dim])
        up = [(i, (i + 1) % size) for i in range(size - 1)]
        down = [(j, i) for i, j in up]
        last = lax.slice_in_dim(x, length - width, length, axis=dim)
        initial = lax.slice_in_dim(x, 0, width, axis=dim)
        before = lax.ppermute(last, axis, up)
        after = lax.ppermute(initial, axis, down)
        x = jnp.concatenate([before, x, after], axis=dim)
    return x


def remesh_kernel(shift):
    mag = jnp.abs(shift)
    inner = 1.0 - 2.5 * mag * mag + 1.5 * mag * mag * mag
    outer = 0.5 * (2.0 - mag) * (2.0 - mag) * (1.0 - mag)
    return jnp.where(mag < 1.0, inner, jnp.where(mag < 2.0, outer, 0.0))


def shifted(padded, axis, offset):
    index = []
    for dim in range(4):
        if dim == 0:
            index.append(slice(None))
        elif dim == axis:
            index.append(slice(offset, offset + padded.shape[dim] - 4))
        else:
            index.append(slice(2, padded.shape[dim] - 2))
    return padded[tuple(index)]


def centered_first(padded, axis):
    return (
        shifted(padded, axis, 0)
        - 8.0 * shifted(padded, axis, 1)
        + 8.0 * shifted(padded, axis, 3)
        - shifted(padded, axis, 4)
    ) / 12.0


def centered_second(padded, axis):
    return (
        -shifted(padded, axis, 0)
        + 16.0 * shifted(padded, axis, 1)
        - 30.0 * shifted(padded, axis, 2)
        + 16.0 * shifted(padded, axis, 3)
        - shifted(padded, axis, 4)
    ) / 12.0


def remesh_padded(field, displace, axis):
    length = field.shape[axis] - 4
    total = jnp.zeros(field.shape[:axis] + (length,) + field.shape[axis + 1 :], jnp.float32)
    for offset in range(-2, 3):
        start = 2 - offset
        part = lax.slice_in_dim(field, start, start + length, axis=axis)
        moved = lax.slice_in_dim(displace, start, start + length, axis=axis - 1)
        total = total + remesh_kernel(offset - moved)[None] * part
    return total


def blade_forces(point_velocity, chord, twist, angle_step):
    count = point_velocity.shape[1]
    points = jnp.arange(count, dtype=jnp.int32)
    station = points % BP
    blade = points // BP % BLADES
    theta = angle_step[0].astype(
        jnp.float32
    ) * turn_step + 2.0 * 3.141592653589793 / 3.0 * blade.astype(jnp.float32)
    radius = (station.astype(jnp.float32) + 0.5) / BP
    cos_t = jnp.cos(theta)
    sin_t = jnp.sin(theta)
    rel_x = point_velocity[0]
    rel_y = point_velocity[1] + tip_speed * radius * sin_t
    rel_z = point_velocity[2] - tip_speed * radius * cos_t
    rel_t = -sin_t * rel_y + cos_t * rel_z
    speed = jnp.sqrt(rel_x * rel_x + rel_t * rel_t + 1.0)
    gamma = 3.141592653589793 * chord * (rel_x * jnp.cos(twist) + rel_t * jnp.sin(twist))
    blades = gamma.reshape(-1, BP)
    before = jnp.concatenate([jnp.zeros((blades.shape[0], 1), jnp.float32), blades[:, :-1]], axis=1)
    shed = (blades - before).reshape(-1)
    return jnp.stack(
        [
            shed * rel_x / speed,
            gamma * cos_t + shed * rel_y / speed,
            gamma * sin_t + shed * rel_z / speed,
        ]
    )


def point_tables(
    cells,
    fracs,
    owner_span,
    owner_vert,
    span_index,
    vert_index,
    span_cells,
    vert_cells,
    axial_cells,
):
    rows_x = jnp.arange(axial_cells, dtype=jnp.int32)
    rows_y = jnp.arange(span_cells, dtype=jnp.int32)
    rows_z = jnp.arange(vert_cells, dtype=jnp.int32)
    gap_x = rows_x[:, None] - cells[0][None, :]
    gap_y = (
        span_index * span_cells
        + rows_y[:, None]
        - owner_span[None, :] * span_cells
        - cells[1][None, :]
    )
    gap_z = (
        vert_index * vert_cells
        + rows_z[:, None]
        - owner_vert[None, :] * vert_cells
        - cells[2][None, :]
    )
    table_x = remesh_kernel(gap_x.astype(jnp.float32) - fracs[0][None, :])
    table_y = remesh_kernel(gap_y.astype(jnp.float32) - fracs[1][None, :])
    table_z = remesh_kernel(gap_z.astype(jnp.float32) - fracs[2][None, :])
    return (table_x, table_y, table_z)


def on_device(omega, velocity, point_owner, point_cells, point_frac, chord, twist, angle_step):
    span_cells, vert_cells, axial_cells = (omega.shape[1], omega.shape[2], omega.shape[3])
    span_count = lax.axis_size("gy")
    vert_count = lax.axis_size("gz")
    span_index = lax.axis_index("gy")
    vert_index = lax.axis_index("gz")
    owner_span = point_owner // vert_count
    owner_vert = point_owner % vert_count
    highest = lax.Precision.HIGHEST
    busiest = 2 * (BLADES * BP) // (span_count // TURBINES * max(vert_count // 2, 1))
    my_block = span_index * vert_count + vert_index
    points = jnp.arange(point_owner.shape[0], dtype=jnp.int32)
    ranking = jnp.where(point_owner == my_block, points, points + point_owner.shape[0])
    picked = jnp.argsort(ranking, stable=True)[:busiest]
    selector = (picked[:, None] == points[None, :]).astype(jnp.float32)
    table_x, table_y, table_z = point_tables(
        point_cells[:, picked],
        point_frac[:, picked],
        owner_span[picked],
        owner_vert[picked],
        span_index,
        vert_index,
        span_cells,
        vert_cells,
        axial_cells,
    )
    columns = jnp.dot(
        velocity.reshape(-1, axial_cells),
        table_x,
        precision=highest,
        preferred_element_type=jnp.float32,
    )
    columns = columns.reshape(3, span_cells, vert_cells, -1)
    compact = jnp.einsum("cyzq,yq,zq->cq", columns, table_y, table_z, precision=highest)
    partial_velocity = jnp.dot(
        compact, selector, precision=highest, preferred_element_type=jnp.float32
    )
    point_velocity = lax.psum(partial_velocity, ("gy", "gz"))
    sources = blade_forces(point_velocity, chord, twist, angle_step)
    local_sources = sources[:, picked]
    spread = jnp.einsum("cq,yq,zq->cyzq", local_sources, table_y, table_z, precision=highest)
    smear = jnp.dot(
        spread.reshape(-1, spread.shape[3]),
        table_x.T,
        precision=highest,
        preferred_element_type=jnp.float32,
    )
    smear = smear.reshape(3, span_cells, vert_cells, axial_cells)
    omega_rim, velocity_rim = (
        with_halo(omega, (("gy", 1), ("gz", 2)), 2),
        with_halo(velocity, (("gy", 1), ("gz", 2)), 2),
    )
    axial_pads = ((0, 0), (0, 0), (0, 0), (2, 2))
    omega_pad = jnp.pad(omega_rim, axial_pads)
    velocity_pad = jnp.pad(velocity_rim, axial_pads)
    stretch = jnp.zeros_like(omega)
    laplace = jnp.zeros_like(omega)
    for axis in range(3):
        stretch = stretch + omega[2 - axis][None] * centered_first(velocity_pad, 3 - axis)
        laplace = laplace + centered_second(omega_pad, axis + 1)
    section = omega + section_step * (stretch + viscosity * laplace + smear)
    shift_x = jnp.clip(section_step * velocity[0], -1.0, 1.0)
    moved_x = remesh_padded(
        jnp.pad(section, axial_pads), jnp.pad(shift_x, ((0, 0), (0, 0), (2, 2))), 3
    )
    shift_z = jnp.clip(section_step * velocity_rim[2][2 : span_cells + 2, :, :], -1.0, 1.0)
    span_rim = with_halo(moved_x, (("gy", 1),), 2)
    shift_y = jnp.clip(section_step * velocity_rim[1][:, 2 : vert_cells + 2, :], -1.0, 1.0)
    moved_mid = remesh_padded(span_rim, shift_y, 1)
    moved_y = with_halo(moved_mid, (("gz", 2),), 2)
    omega_out = remesh_padded(moved_y, shift_z, 2)
    return (omega_out, sources)


def solution(mesh):
    in_specs = (P(None, "gy", "gz", None), P(None, "gy", "gz", None), P(), P(), P(), P(), P(), P())
    out_specs = (P(None, "gy", "gz", None), P())
    return jax.shard_map(
        on_device, mesh=mesh, in_specs=in_specs, out_specs=out_specs, check_vma=False
    )
```

profile of v0, /device:TPU:6, one launch (start us, length us, event | category | flops | bytes accessed | tf_op | source)
XLA Modules:
  0.0 162.9 jit_solution(6236119518289551892)
XLA Ops:
  0.6 1.8 %fusion.252 = (f32[3,2,64,128]{3,2,1,0:T(8,128)}, f32[3,2,64,128]{3,2,1,0:T(8,128)}) fusion(f32[3,16,64,128]{3,2,1,0:T(8,128)} %param.9), kind=kLoop, calls=%fused_computation.439 | loop fusion | bytes 786432 | tf_op jit(solution)/shard_map/slice | solution.py:23
  2.5 2.0 %collective-permute-start = (f32[3,2,64,128]{3,2,1,0:T(8,128)}, f32[3,2,64,128]{3,2,1,0:T(8,128)}, u32[]{:S(2)}, u32[]{:S(2)}) collective-permute-start(f32[3,2,64,128]{3,2,1,0:T(8,128)} %get-tuple-element.33), channel_id=1, source_target_pairs={{0,2},{2,4},{4,6},{6,8},{8,10},{10,12},{12,14},{14,16},{16,18},{18... | collective-permute-start | bytes 589832 | tf_op jit(solution)/shard_map/ppermute | solution.py:24
  4.5 3.6 %collective-permute-start.1 = (f32[3,2,64,128]{3,2,1,0:T(8,128)}, f32[3,2,64,128]{3,2,1,0:T(8,128)}, u32[]{:S(2)}, u32[]{:S(2)}) collective-permute-start(f32[3,2,64,128]{3,2,1,0:T(8,128)} %get-tuple-element.32), channel_id=1, source_target_pairs={{2,0},{4,2},{6,4},{8,6},{10,8},{12,10},{14,12},{16,14},{18,16},{20... | collective-permute-start | bytes 589832 | tf_op jit(solution)/shard_map/ppermute | solution.py:25
  8.2 1.7 %fusion.253 = (f32[3,2,64,128]{3,2,1,0:T(8,128)S(1)}, f32[3,2,64,128]{3,2,1,0:T(8,128)}) fusion(f32[3,16,64,128]{3,2,1,0:T(8,128)} %param.8), kind=kLoop, calls=%fused_computation.440 | loop fusion | bytes 786432 | tf_op jit(solution)/shard_map/slice | solution.py:23
  9.9 2.0 %collective-permute-start.4 = (f32[3,2,64,128]{3,2,1,0:T(8,128)}, f32[3,2,64,128]{3,2,1,0:T(8,128)}, u32[]{:S(2)}, u32[]{:S(2)}) collective-permute-start(f32[3,2,64,128]{3,2,1,0:T(8,128)} %get-tuple-element.35), channel_id=1, source_target_pairs={{0,2},{2,4},{4,6},{6,8},{8,10},{10,12},{12,14},{14,16},{16,18},{18... | collective-permute-start | bytes 589832 | tf_op jit(solution)/shard_map/ppermute | solution.py:24
  11.9 3.6 %collective-permute-start.5 = (f32[3,2,64,128]{3,2,1,0:T(8,128)S(1)}, f32[3,2,64,128]{3,2,1,0:T(8,128)}, u32[]{:S(2)}, u32[]{:S(2)}) collective-permute-start(f32[3,2,64,128]{3,2,1,0:T(8,128)S(1)} %get-tuple-element.34), channel_id=1, source_target_pairs={{2,0},{4,2},{6,4},{8,6},{10,8},{12,10},{14,12},{16,14},{18,16},{20... | collective-permute-start | bytes 589832 | tf_op jit(solution)/shard_map/ppermute | solution.py:25
  15.6 5.0 %sort.17 = (s32[1152]{0:T(1024)}, s32[1152]{0:T(1024)S(1)}) sort(s32[1152]{0:T(1024)S(1)} %get-tuple-element.63, s32[1152]{0:T(1024)S(1)} %iota.43), dimensions={0}, to_apply=%region_0.1 | sort | flops 12672 | bytes 18432 | tf_op jit(solution)/shard_map/jit(argsort)/sort | solution.py:154
  20.7 1.4 gather_fusion.3
  22.4 0.7 gather_fusion.1
  23.7 0.7 gather_fusion.2
  25.2 3.6 %convolution_bitcast_fusion = f32[3072,192]{0,1:T(8,128)} fusion(f32[3072,128]{1,0:T(8,128)S(1)} %bitcast.49, f32[192]{0:T(256)S(1)} %get-tuple-element.8, s32[192]{0:T(256)S(1)} %get-tuple-element.5), kind=kOutput, calls=%fused_computation.18 | convolution fusion | flops 906461184 | bytes 3933696 | tf_op jit(solution)/shard_map/dot_general | solution.py:167
  28.8 2.2 %copy.29 = f32[3072,192]{1,0:T(8,128)S(1)} copy(f32[3072,192]{0,1:T(8,128)} %convolution_bitcast_fusion) | data formatting | bytes 4718592
  31.9 1.4 gather_fusion
  33.5 1.4 fusion.255
  35.4 42.3 %psum.7 = f32[3,1152]{1,0:T(4,128)S(1)} all-reduce(f32[3,1152]{1,0:T(4,128)S(1)} %fusion.77), channel_id=1, replica_groups=mesh['gy'=16,'gz'=2] {'gy','gz'}, use_global_device_ids=true, to_apply=%region_1.2 | all-reduce | flops 3456 | bytes 27648 | tf_op jit(solution)/shard_map/psum | solution.py:178
  78.8 1.2 multiply_bitcast_fusion.2
  80.0 0.8 copy-done.1
  80.8 1.3 fusion.104
  82.5 1.1 copy.17
  83.5 1.7 %gather_fusion.4 = f32[192,3]{1,0:T(8,128)S(1)} fusion(f32[3,1152]{0,1:T(8,128)} %copy.17, s32[1024]{0:T(1024)S(1)} %pad_clamp_fusion), kind=kCustom, calls=%fused_computation.4 | custom fusion | bytes 5376 | tf_op jit(solution)/shard_map/gather | solution.py:180
  85.4 4.3 %fusion.93 = (f32[16,64,128]{2,1,0:T(8,128)}, f32[16,64,128]{2,1,0:T(8,128)}, f32[16,64,128]{2,1,0:T(8,128)}, f32[16,64,128]{2,1,0:T(8,128)}) fusion(f32[16,64,128]{2,1,0:T(8,128)} %get-tuple-element.22), kind=kLoop, calls=%fused_computation.199 | loop fusion | flops 9437184 | bytes 2621440 | tf_op jit(solution)/shard_map/jit(_where)/select_n | solution.py:34
  89.7 0.6 broadcast_multiply_fusion
  90.3 1.0 constant_dynamic-update-slice_fusion.4
  91.3 0.6 constant_dynamic-update-slice_fusion.3
  91.9 1.2 constant_dynamic-update-slice_fusion.5
  93.1 1.3 collective-permute-start.2
  94.4 4.7 %collective-permute-start.3 = (f32[3,20,2,128]{3,2,1,0:T(2,128)S(1)}, f32[3,20,2,128]{3,2,1,0:T(2,128)S(1)}, u32[]{:S(2)}, u32[]{:S(2)}) collective-permute-start(f32[3,20,2,128]{3,2,1,0:T(2,128)S(1)} %get-tuple-element.14), channel_id=1, source_target_pairs={{1,0},{3,2},{5,4},{7,6},{9,8},{11,10},{13,12},{15,14},{17,16},{19,... | collective-permute-start | bytes 184328 | tf_op jit(solution)/shard_map/ppermute | solution.py:25
  99.2 1.0 constant_dynamic-update-slice_fusion.8
  100.2 0.6 constant_dynamic-update-slice_fusion.7
  100.8 1.2 constant_dynamic-update-slice_fusion.9
  102.1 1.3 collective-permute-start.6
  103.4 4.5 %collective-permute-start.7 = (f32[3,20,2,128]{3,2,1,0:T(2,128)S(1)}, f32[3,20,2,128]{3,2,1,0:T(2,128)S(1)}, u32[]{:S(2)}, u32[]{:S(2)}) collective-permute-start(f32[3,20,2,128]{3,2,1,0:T(2,128)S(1)} %get-tuple-element.16), channel_id=1, source_target_pairs={{1,0},{3,2},{5,4},{7,6},{9,8},{11,10},{13,12},{15,14},{17,16},{19,... | collective-permute-start | bytes 184328 | tf_op jit(solution)/shard_map/ppermute | solution.py:25
  107.9 1.7 %pad_maximum_fusion = f32[3,20,68,128]{3,2,1,0:T(8,128)} fusion(f32[3,20,2,128]{3,2,1,0:T(2,128)S(1)} %collective-permute-done.3, f32[3,20,64,128]{3,2,1,0:T(8,128)S(1)} %get-tuple-element.53, f32[3,20,2,128]{3,2,1,0:T(2,128)S(1)} %collective-permute-done.2), kind=kLoop, calls=%fused_computation.23 | loop fusion | flops 1044480 | bytes 4177920 | tf_op jit(solution)/shard_map/concatenate | solution.py:26
  109.7 1.2 slice_bitcast_fusion
  110.9 3.5 %select_maximum_fusion = f32[3,20,68,132]{3,2,1,0:T(8,128)} fusion(f32[3,20,2,128]{3,2,1,0:T(2,128)S(1)} %collective-permute-done.7, f32[3,20,64,128]{3,2,1,0:T(8,128)S(1)} %get-tuple-element.57, f32[3,20,2,128]{3,2,1,0:T(2,128)S(1)} %collective-permute-done.6), kind=kLoop, calls=%fused_computation.15 | loop fusion | flops 4308480 | bytes 4243200 | tf_op jit(solution)/shard_map/concatenate | solution.py:26
  114.5 20.4 %fusion.30 = f32[3,16,64,128]{3,2,1,0:T(8,128)} fusion(f32[3,16,64,128]{3,2,1,0:T(8,128)S(1)} %copy-done.2, f32[3,20,64,128]{3,2,1,0:T(8,128)} %copy-done.4, f32[3,20,2,128]{3,2,1,0:T(2,128)S(1)} %collective-permute-done.7, f32[3,20,2,128]{3,2,1,0:T(2,128)S(1)} %collective-permute-done.6, f32[3,20,64,128]{3,2,1,0:T(8,128)} %copy-done.3, ...), kind=kOutput, calls=%fused_computation.70 | convolution fusion | flops 929464320 | bytes 29947392 | tf_op jit(solution)/shard_map/dot_general | solution.py:182
  134.8 6.4 %fusion.48 = f32[3,16,64,128]{3,2,1,0:T(8,128)S(1)} fusion(f32[3,16,64,128]{3,2,1,0:T(8,128)} %fusion.30, f32[16,64,128]{2,1,0:T(8,128)} %get-tuple-element.49, f32[16,64,128]{2,1,0:T(8,128)} %get-tuple-element.48, f32[16,64,128]{2,1,0:T(8,128)S(1)} %copy-done.5, f32[16,64,128]{2,1,0:T(8,128)} %get-tuple-element.47, f32[16,64,128]{2,1,0:T(8,128)} %get-tuple-element.46), kind=kLoop, calls=%fused_computation.88 | loop fusion | flops 3538944 | bytes 5767168 | tf_op jit(solution)/shard_map/add | solution.py:75
  141.3 1.9 %collective-permute-start.8 = (f32[3,2,64,128]{3,2,1,0:T(8,128)S(1)}, f32[3,2,64,128]{3,2,1,0:T(8,128)S(1)}, u32[]{:S(2)}, u32[]{:S(2)}) collective-permute-start(f32[3,2,64,128]{3,2,1,0:T(8,128)S(1)} %get-tuple-element.19), channel_id=1, source_target_pairs={{2,0},{4,2},{6,4},{8,6},{10,8},{12,10},{14,12},{16,14},{18,16},{20... | collective-permute-start | bytes 589832 | tf_op jit(solution)/shard_map/ppermute | solution.py:25
  143.2 2.4 %collective-permute-start.9 = (f32[3,2,64,128]{3,2,1,0:T(8,128)S(1)}, f32[3,2,64,128]{3,2,1,0:T(8,128)S(1)}, u32[]{:S(2)}, u32[]{:S(2)}) collective-permute-start(f32[3,2,64,128]{3,2,1,0:T(8,128)S(1)} %get-tuple-element.20), channel_id=1, source_target_pairs={{0,2},{2,4},{4,6},{6,8},{8,10},{10,12},{12,14},{14,16},{16,18},{18... | collective-permute-start | bytes 589832 | tf_op jit(solution)/shard_map/ppermute | solution.py:24
  145.7 1.5 fusion.88
  147.3 1.1 fusion.80
  148.4 2.0 %collective-permute-done.9 = f32[3,2,64,128]{3,2,1,0:T(8,128)S(1)} collective-permute-done((f32[3,2,64,128]{3,2,1,0:T(8,128)S(1)}, f32[3,2,64,128]{3,2,1,0:T(8,128)S(1)}, u32[]{:S(2)}, u32[]{:S(2)}) %collective-permute-start.9) | collective-permute-done | bytes 196640 | tf_op jit(solution)/shard_map/ppermute | solution.py:24
  150.4 1.3 fusion.15
  151.7 3.1 %collective-permute-start.10 = (f32[3,16,2,128]{3,2,1,0:T(2,128)S(1)}, f32[3,16,2,128]{3,2,1,0:T(2,128)S(1)}, u32[]{:S(2)}, u32[]{:S(2)}) collective-permute-start(f32[3,16,2,128]{3,2,1,0:T(2,128)S(1)} %get-tuple-element.17), channel_id=1, source_target_pairs={{1,0},{3,2},{5,4},{7,6},{9,8},{11,10},{13,12},{15,14},{17,16},{19,... | collective-permute-start | bytes 147464 | tf_op jit(solution)/shard_map/ppermute | solution.py:25
  154.8 1.3 collective-permute-start.11
  156.1 1.7 %fusion.83 = (f32[16,64,128]{2,1,0:T(8,128)S(1)}, f32[16,64,128]{2,1,0:T(8,128)S(1)}, f32[16,64,128]{2,1,0:T(8,128)S(1)}, f32[16,64,128]{2,1,0:T(8,128)S(1)}, f32[16,64,128]{2,1,0:T(8,128)S(1)}) fusion(f32[16,68,128]{2,1,0:T(8,128)S(1)} %fusion.80), kind=kLoop, calls=%fused_computation.189 | loop fusion | flops 11796480 | bytes 5242880 | tf_op jit(solution)/shard_map/jit(_where)/select_n | solution.py:34
  157.8 3.0 %collective-permute-done.11 = f32[3,16,2,128]{3,2,1,0:T(2,128)S(1)} collective-permute-done((f32[3,16,2,128]{3,2,1,0:T(2,128)S(1)}, f32[3,16,2,128]{3,2,1,0:T(2,128)S(1)}, u32[]{:S(2)}, u32[]{:S(2)}) %collective-permute-start.11) | collective-permute-done | bytes 49184 | tf_op jit(solution)/shard_map/ppermute | solution.py:24
  160.8 2.1 %fusion.7 = f32[3,16,64,128]{3,2,1,0:T(8,128)} fusion(f32[3,16,2,128]{3,2,1,0:T(2,128)S(1)} %collective-permute-done.11, f32[3,16,64,128]{3,2,1,0:T(8,128)S(1)} %fusion.15, f32[3,16,2,128]{3,2,1,0:T(2,128)S(1)} %collective-permute-done.10, f32[16,64,128]{2,1,0:T(8,128)S(1)} %get-tuple-element.42, f32[16,64,128]{2,1,0:T(8,128)S(1)} %get-tuple-element.43, ...), kind=kLoop, calls=%fused_computation.47 | loop fusion | flops 5111808 | bytes 5865472 | tf_op jit(solution)/shard_map/add | solution.py:75
  (86 shorter events, 4.2 us)
Async XLA Ops:
  0.6 15.0 %copy-start.16 = (s32[1152]{0:T(1024)S(1)}, s32[1152]{0:T(1024)}, u32[]{:S(2)}) copy-start(s32[1152]{0:T(1024)} %param.10) | copy-start | bytes 13828
  0.6 21.5 %copy-start.12 = (s32[3,1152]{1,0:T(4,128)S(1)}, s32[3,1152]{1,0:T(4,128)}, u32[]{:S(2)}) copy-start(s32[3,1152]{1,0:T(4,128)} %param.11) | copy-start | bytes 41476
  2.5 21.0 %copy-start.13 = (f32[3,1152]{1,0:T(4,128)S(1)}, f32[3,1152]{1,0:T(4,128)}, u32[]{:S(2)}) copy-start(f32[3,1152]{1,0:T(4,128)} %param.12) | copy-start | bytes 41476
  2.5 87.8 %collective-permute-start = (f32[3,2,64,128]{3,2,1,0:T(8,128)}, f32[3,2,64,128]{3,2,1,0:T(8,128)}, u32[]{:S(2)}, u32[]{:S(2)}) collective-permute-start(f32[3,2,64,128]{3,2,1,0:T(8,128)} %get-tuple-element.33), channel_id=1, source_target_pairs={{0,2},{2,4},{4,6},{6,8},{8,10},{10,12},{12,14},{14,16},{16,18},{18... | collective-permute-start | bytes 589832 | tf_op jit(solution)/shard_map/ppermute | solution.py:24
  4.5 87.4 %collective-permute-start.1 = (f32[3,2,64,128]{3,2,1,0:T(8,128)}, f32[3,2,64,128]{3,2,1,0:T(8,128)}, u32[]{:S(2)}, u32[]{:S(2)}) collective-permute-start(f32[3,2,64,128]{3,2,1,0:T(8,128)} %get-tuple-element.32), channel_id=1, source_target_pairs={{2,0},{4,2},{6,4},{8,6},{10,8},{12,10},{14,12},{16,14},{18,16},{20... | collective-permute-start | bytes 589832 | tf_op jit(solution)/shard_map/ppermute | solution.py:25
  9.9 15.3 %copy-start = (f32[3,16,64,128]{3,2,1,0:T(8,128)S(1)}, f32[3,16,64,128]{3,2,1,0:T(8,128)}, u32[]{:S(2)}) copy-start(f32[3,16,64,128]{3,2,1,0:T(8,128)} %param.9) | copy-start | bytes 4718596
  9.9 89.3 %collective-permute-start.4 = (f32[3,2,64,128]{3,2,1,0:T(8,128)}, f32[3,2,64,128]{3,2,1,0:T(8,128)}, u32[]{:S(2)}, u32[]{:S(2)}) collective-permute-start(f32[3,2,64,128]{3,2,1,0:T(8,128)} %get-tuple-element.35), channel_id=1, source_target_pairs={{0,2},{2,4},{4,6},{6,8},{8,10},{10,12},{12,14},{14,16},{16,18},{18... | collective-permute-start | bytes 589832 | tf_op jit(solution)/shard_map/ppermute | solution.py:24
  11.9 88.8 %collective-permute-start.5 = (f32[3,2,64,128]{3,2,1,0:T(8,128)S(1)}, f32[3,2,64,128]{3,2,1,0:T(8,128)}, u32[]{:S(2)}, u32[]{:S(2)}) collective-permute-start(f32[3,2,64,128]{3,2,1,0:T(8,128)S(1)} %get-tuple-element.34), channel_id=1, source_target_pairs={{2,0},{4,2},{6,4},{8,6},{10,8},{12,10},{14,12},{16,14},{18,16},{20... | collective-permute-start | bytes 589832 | tf_op jit(solution)/shard_map/ppermute | solution.py:25
  23.4 1.3 copy-start.17
  24.7 0.6 copy-start.19
  31.6 46.8 %copy-start.14 = (f32[1152]{0:T(1024)S(1)}, f32[1152]{0:T(1024)}, u32[]{:S(2)}) copy-start(f32[1152]{0:T(1024)} %param.14) | copy-start | bytes 13828
  31.6 46.8 %copy-start.15 = (f32[1152]{0:T(1024)S(1)}, f32[1152]{0:T(1024)}, u32[]{:S(2)}) copy-start(f32[1152]{0:T(1024)} %param.13) | copy-start | bytes 13828
  31.6 47.2 %copy-start.2 = (f32[3,16,64,128]{3,2,1,0:T(8,128)S(1)}, f32[3,16,64,128]{3,2,1,0:T(8,128)}, u32[]{:S(2)}) copy-start(f32[3,16,64,128]{3,2,1,0:T(8,128)} %param.8) | copy-start | bytes 4718596
  78.8 2.0 %copy-start.1 = (f32[3,16,64,128]{3,2,1,0:T(8,128)S(1)}, f32[3,16,64,128]{3,2,1,0:T(8,128)}, u32[]{:S(2)}) copy-start(f32[3,16,64,128]{3,2,1,0:T(8,128)} %param.9) | copy-start | bytes 4718596
  82.4 7.2 %copy-start.8 = (f32[3,1152]{1,0:T(4,128)}, f32[3,1152]{1,0:T(4,128)S(1)}, u32[]{:S(2)}) copy-start(f32[3,1152]{1,0:T(4,128)S(1)} %pad_maximum_fusion.9) | copy-start | bytes 41476
  91.8 7.3 %copy-start.10 = (f32[3,18,64,128]{3,2,1,0:T(8,128)}, f32[3,18,64,128]{3,2,1,0:T(8,128)S(1)}, u32[]{:S(2)}) copy-start(f32[3,18,64,128]{3,2,1,0:T(8,128)S(1)} %get-tuple-element.26) | copy-start | bytes 5308420
  93.1 6.1 %copy-start.6 = (f32[3,18,64,128]{3,2,1,0:T(8,128)}, f32[3,18,64,128]{3,2,1,0:T(8,128)S(1)}, u32[]{:S(2)}) copy-start(f32[3,18,64,128]{3,2,1,0:T(8,128)S(1)} %get-tuple-element.52) | copy-start | bytes 5308420
  93.1 16.6 %copy-start.3 = (f32[3,20,64,128]{3,2,1,0:T(8,128)}, f32[3,20,64,128]{3,2,1,0:T(8,128)S(1)}, u32[]{:S(2)}) copy-start(f32[3,20,64,128]{3,2,1,0:T(8,128)S(1)} %get-tuple-element.53) | copy-start | bytes 5898244
  93.1 14.8 %collective-permute-start.2 = (f32[3,20,2,128]{3,2,1,0:T(2,128)S(1)}, f32[3,20,2,128]{3,2,1,0:T(2,128)S(1)}, u32[]{:S(2)}, u32[]{:S(2)}) collective-permute-start(f32[3,20,2,128]{3,2,1,0:T(2,128)S(1)} %get-tuple-element.13), channel_id=1, source_target_pairs={{0,1},{2,3},{4,5},{6,7},{8,9},{10,11},{12,13},{14,15},{16,17},{18,... | collective-permute-start | bytes 184328 | tf_op jit(solution)/shard_map/ppermute | solution.py:24
  94.4 13.5 %collective-permute-start.3 = (f32[3,20,2,128]{3,2,1,0:T(2,128)S(1)}, f32[3,20,2,128]{3,2,1,0:T(2,128)S(1)}, u32[]{:S(2)}, u32[]{:S(2)}) collective-permute-start(f32[3,20,2,128]{3,2,1,0:T(2,128)S(1)} %get-tuple-element.14), channel_id=1, source_target_pairs={{1,0},{3,2},{5,4},{7,6},{9,8},{11,10},{13,12},{15,14},{17,16},{19,... | collective-permute-start | bytes 184328 | tf_op jit(solution)/shard_map/ppermute | solution.py:25
  100.8 13.7 %copy-start.11 = (f32[3,18,64,128]{3,2,1,0:T(8,128)}, f32[3,18,64,128]{3,2,1,0:T(8,128)S(1)}, u32[]{:S(2)}) copy-start(f32[3,18,64,128]{3,2,1,0:T(8,128)S(1)} %get-tuple-element.29) | copy-start | bytes 5308420
  102.0 7.7 %copy-start.7 = (f32[3,18,64,128]{3,2,1,0:T(8,128)}, f32[3,18,64,128]{3,2,1,0:T(8,128)S(1)}, u32[]{:S(2)}) copy-start(f32[3,18,64,128]{3,2,1,0:T(8,128)S(1)} %get-tuple-element.56) | copy-start | bytes 5308420
  102.0 8.9 %copy-start.4 = (f32[3,20,64,128]{3,2,1,0:T(8,128)}, f32[3,20,64,128]{3,2,1,0:T(8,128)S(1)}, u32[]{:S(2)}) copy-start(f32[3,20,64,128]{3,2,1,0:T(8,128)S(1)} %get-tuple-element.57) | copy-start | bytes 5898244
  102.1 8.8 %collective-permute-start.6 = (f32[3,20,2,128]{3,2,1,0:T(2,128)S(1)}, f32[3,20,2,128]{3,2,1,0:T(2,128)S(1)}, u32[]{:S(2)}, u32[]{:S(2)}) collective-permute-start(f32[3,20,2,128]{3,2,1,0:T(2,128)S(1)} %get-tuple-element.15), channel_id=1, source_target_pairs={{0,1},{2,3},{4,5},{6,7},{8,9},{10,11},{12,13},{14,15},{16,17},{18,... | collective-permute-start | bytes 184328 | tf_op jit(solution)/shard_map/ppermute | solution.py:24
  103.4 7.5 %collective-permute-start.7 = (f32[3,20,2,128]{3,2,1,0:T(2,128)S(1)}, f32[3,20,2,128]{3,2,1,0:T(2,128)S(1)}, u32[]{:S(2)}, u32[]{:S(2)}) collective-permute-start(f32[3,20,2,128]{3,2,1,0:T(2,128)S(1)} %get-tuple-element.16), channel_id=1, source_target_pairs={{1,0},{3,2},{5,4},{7,6},{9,8},{11,10},{13,12},{15,14},{17,16},{19,... | collective-permute-start | bytes 184328 | tf_op jit(solution)/shard_map/ppermute | solution.py:25
  110.9 3.6 %copy-start.9 = (f32[192,16,3]{0,1,2:T(8,128)S(1)}, f32[192,16,3]{0,1,2:T(8,128)}, u32[]{:S(2)}) copy-start(f32[192,16,3]{0,1,2:T(8,128)} %broadcast_multiply_fusion) | copy-start | bytes 110596
  110.9 3.6 %copy-start.18 = (s32[192]{0:T(256)S(1)}, s32[192]{0:T(256)}, u32[]{:S(2)}) copy-start(s32[192]{0:T(256)} %copy-done.17) | copy-start | bytes 2308
  110.9 3.6 %copy-start.20 = (f32[192]{0:T(256)S(1)}, f32[192]{0:T(256)}, u32[]{:S(2)}) copy-start(f32[192]{0:T(256)} %copy-done.19) | copy-start | bytes 2308
  114.4 20.4 %copy-start.5 = (f32[16,64,128]{2,1,0:T(8,128)S(1)}, f32[16,64,128]{2,1,0:T(8,128)}, u32[]{:S(2)}) copy-start(f32[16,64,128]{2,1,0:T(8,128)} %get-tuple-element.21) | copy-start | bytes 1572868
  141.3 7.1 %collective-permute-start.8 = (f32[3,2,64,128]{3,2,1,0:T(8,128)S(1)}, f32[3,2,64,128]{3,2,1,0:T(8,128)S(1)}, u32[]{:S(2)}, u32[]{:S(2)}) collective-permute-start(f32[3,2,64,128]{3,2,1,0:T(8,128)S(1)} %get-tuple-element.19), channel_id=1, source_target_pairs={{2,0},{4,2},{6,4},{8,6},{10,8},{12,10},{14,12},{16,14},{18,16},{20... | collective-permute-start | bytes 589832 | tf_op jit(solution)/shard_map/ppermute | solution.py:25
  143.2 7.2 %collective-permute-start.9 = (f32[3,2,64,128]{3,2,1,0:T(8,128)S(1)}, f32[3,2,64,128]{3,2,1,0:T(8,128)S(1)}, u32[]{:S(2)}, u32[]{:S(2)}) collective-permute-start(f32[3,2,64,128]{3,2,1,0:T(8,128)S(1)} %get-tuple-element.20), channel_id=1, source_target_pairs={{0,2},{2,4},{4,6},{6,8},{8,10},{10,12},{12,14},{14,16},{16,18},{18... | collective-permute-start | bytes 589832 | tf_op jit(solution)/shard_map/ppermute | solution.py:24
  151.7 6.1 %collective-permute-start.10 = (f32[3,16,2,128]{3,2,1,0:T(2,128)S(1)}, f32[3,16,2,128]{3,2,1,0:T(2,128)S(1)}, u32[]{:S(2)}, u32[]{:S(2)}) collective-permute-start(f32[3,16,2,128]{3,2,1,0:T(2,128)S(1)} %get-tuple-element.17), channel_id=1, source_target_pairs={{1,0},{3,2},{5,4},{7,6},{9,8},{11,10},{13,12},{15,14},{17,16},{19,... | collective-permute-start | bytes 147464 | tf_op jit(solution)/shard_map/ppermute | solution.py:25
  154.8 6.0 %collective-permute-start.11 = (f32[3,16,2,128]{3,2,1,0:T(2,128)S(1)}, f32[3,16,2,128]{3,2,1,0:T(2,128)S(1)}, u32[]{:S(2)}, u32[]{:S(2)}) collective-permute-start(f32[3,16,2,128]{3,2,1,0:T(2,128)S(1)} %get-tuple-element.18), channel_id=1, source_target_pairs={{0,1},{2,3},{4,5},{6,7},{8,9},{10,11},{12,13},{14,15},{16,17},{18,... | collective-permute-start | bytes 147464 | tf_op jit(solution)/shard_map/ppermute | solution.py:24
where the time goes:
time: 164 us; the launch traced here: 163 us
  blocking collectives  42.3 us (26%)
  other arithmetic  33.1 us (20%)
  starting transfers between devices  32 us (20%)
  matrix products  25.8 us (16%)
  local copies, waits for them, and re-layouts  22.7 us (14%)
  waiting for transfers between devices  5.01 us (3%)
  between operations  2 us (1%)
    psum x1, blocking collectives, on_device(): point_velocity = lax.psum(partial_velocity, ('gy', 'gz'))  42.3 us
    ppermute x6, starting transfers between devices, with_halo(): after = lax.ppermute(initial, axis, down)  21.6 us
    dot_general x1, matrix products, on_device(): jnp.dot(spread.reshape(-1, spread.shape[3]), table_x.T, precision=highest...  20.4 us
    ppermute x6, starting transfers between devices, with_halo(): before = lax.ppermute(last, axis, up)  10.4 us
    add x3, other arithmetic, remesh_padded(): total = total + remesh_kernel(offset - moved)[None] * part  9.8 us
    select_n x4, other arithmetic, remesh_kernel(): return jnp.where(mag < 1.0, inner, jnp.where(mag < 2.0, outer, 0.0))  7.58 us
    unnamed x47, local copies, waits for them, and re-layouts  6.02 us
    concatenate x2, other arithmetic, with_halo(): x = jnp.concatenate([before, x, after], axis=dim)  5.26 us
  transfers between devices with their start and end apart: 12, of which 2 were waited for; matrix products, arithmetic and copies ran while one was open for 27% of the time, Pallas kernels for 0%

commit v1 on v0

v1 whole, which is shorter than its diff:
```python
import functools

import jax
import jax.numpy as jnp
from jax import lax
from jax.experimental import pallas as pl
from jax.experimental.pallas import tpu as pltpu
from jax.sharding import PartitionSpec as P

TURBINES = 6
BLADES = 3
BP = 64
ROTOR = BLADES * BP
LANES = 128
WINDOW = 256

section_step = 0.4
viscosity = 0.05
tip_speed = 3.0
turn_step = 2.0 * 3.141592653589793 / 720.0
pi = 3.141592653589793

MESH = pl.DeviceIdType.MESH


def remesh_kernel(shift):
    mag = jnp.abs(shift)
    inner = 1.0 - mag * mag * (2.5 - 1.5 * mag)
    outer = 0.5 * (2.0 - mag) * (2.0 - mag) * (1.0 - mag)
    return jnp.where(mag < 1.0, inner, jnp.where(mag < 2.0, outer, 0.0))


def tap_weights(speed):
    d = jnp.clip(section_step * speed, -1.0, 1.0)
    t = jnp.abs(d)
    t2 = t * t
    h = 0.5 * t2 * t
    centre = 1.0 - 2.5 * t2 + 3.0 * h
    toward = 0.5 * t + 2.0 * t2 - 3.0 * h
    away = t2 - 0.5 * t - h
    far = h - 0.5 * t2
    right = d > 0.0
    zero = jnp.zeros_like(d)
    return (
        jnp.where(right, zero, far),
        jnp.where(right, away, toward),
        centre,
        jnp.where(right, toward, away),
        jnp.where(right, far, zero),
    )


def blade_forces(vel, chord, twist, angle, first, count):
    points = first + lax.broadcasted_iota(jnp.int32, (1, count), 1)
    station = points % BP
    blade = points // BP % BLADES
    row = lax.broadcasted_iota(jnp.int32, (8, LANES), 0).astype(jnp.float32)
    theta = angle.astype(jnp.float32) * turn_step + 2.0 * pi / 3.0 * row
    cos_r = jnp.cos(theta)
    sin_r = jnp.sin(theta)
    cos_t = jnp.where(blade == 0, cos_r[0:1, 0:1], jnp.where(blade == 1, cos_r[1:2, 0:1], cos_r[2:3, 0:1]))
    sin_t = jnp.where(blade == 0, sin_r[0:1, 0:1], jnp.where(blade == 1, sin_r[1:2, 0:1], sin_r[2:3, 0:1]))
    radius = (station.astype(jnp.float32) + 0.5) / BP
    rel_x = vel[0]
    rel_y = vel[1] + tip_speed * radius * sin_t
    rel_z = vel[2] - tip_speed * radius * cos_t
    rel_t = -sin_t * rel_y + cos_t * rel_z
    speed = jnp.sqrt(rel_x * rel_x + rel_t * rel_t + 1.0)
    gamma = pi * chord * (rel_x * jnp.cos(twist) + rel_t * jnp.sin(twist))
    before = jnp.where(station == 0, 0.0, pltpu.roll(gamma, 1, 1))
    shed = (gamma - before) / speed
    return (shed * rel_x, gamma * cos_t + shed * rel_y, gamma * sin_t + shed * rel_z)


def split(value):
    high = value.astype(jnp.bfloat16)
    return high, (value - high.astype(jnp.float32)).astype(jnp.bfloat16)


def dot(a, b):
    return jnp.dot(a, b, preferred_element_type=jnp.float32)


def kernel(
    ny, nz, om, ve, cells, fracs, owner, chord, twist, angle, moved, rim, sources,
    F, M, N, smear, d_x, l_x, s_x, slots, acc, tx_h, tx_l, ty, tz, tt_h, tt_l, srow, zsend, zrecv, wsend, wrecv,
    in_sem, out_sem, rim_sem, y_send, y_recv, z_send, z_recv, v_send, v_recv, w_send, w_recv, s_send, s_recv,
):
    cy, cz, nx = om.shape[1], om.shape[2], om.shape[3]
    gy = lax.axis_index("gy")
    gz = lax.axis_index("gz")
    n = ny * nz
    me = gy * nz + gz
    span_blocks = ny // TURBINES
    vert_blocks = max(nz // 2, 1)
    vert_first = (nz - vert_blocks) // 2
    group = span_blocks * vert_blocks
    has = (gy < span_blocks * TURBINES) & (gz >= vert_first) & (gz < vert_first + vert_blocks)
    rotor = lax.min(gy // span_blocks, TURBINES - 1)
    slot = jnp.clip(
        rotor * group + gy % span_blocks * vert_blocks + gz - vert_first, 0, TURBINES * group - 1
    )
    base = pl.multiple_of((rotor // 2) * (2 * ROTOR) + (rotor % 2) * LANES, LANES)
    lo_y, hi_y, lo_z, hi_z = gy > 0, gy < ny - 1, gz > 0, gz < nz - 1
    zin = pl.ds(8, cz)

    load_o = pltpu.make_async_copy(om, F.at[0:3, pl.ds(2, cy), zin], in_sem.at[0])
    load_v = pltpu.make_async_copy(ve, F.at[3:6, pl.ds(2, cy), zin], in_sem.at[1])
    load_v.start()
    load_o.start()

    barrier = pltpu.get_barrier_semaphore()

    def greet(i, carry):
        d = (me + i) % n
        pl.semaphore_signal(barrier, inc=1, device_id={"gy": d // nz, "gz": d % nz}, device_id_type=MESH)
        return carry

    lax.fori_loop(1, n, greet, 0)

    @pl.when(jnp.logical_not(lo_y))
    def _():
        F[:, 0:2, 8 : 8 + cz] = jnp.zeros((6, 2, cz, nx), jnp.float32)
        M[:, 0:2] = jnp.zeros((3, 2, cz, nx), jnp.float32)

    @pl.when(jnp.logical_not(hi_y))
    def _():
        F[:, cy + 2 : cy + 4, 8 : 8 + cz] = jnp.zeros((6, 2, cz, nx), jnp.float32)
        M[:, cy + 2 : cy + 4] = jnp.zeros((3, 2, cz, nx), jnp.float32)

    @pl.when(jnp.logical_not(lo_z))
    def _():
        zrecv[0] = jnp.zeros(zrecv.shape[1:], jnp.float32)
        wrecv[0] = jnp.zeros(wrecv.shape[1:], jnp.float32)

    @pl.when(jnp.logical_not(hi_z))
    def _():
        zrecv[1] = jnp.zeros(zrecv.shape[1:], jnp.float32)
        wrecv[1] = jnp.zeros(wrecv.shape[1:], jnp.float32)

    gap = lax.broadcasted_iota(jnp.int32, (nx, nx), 0) - lax.broadcasted_iota(jnp.int32, (nx, nx), 1)

    def banded(values):
        total = jnp.zeros((nx, nx), jnp.float32)
        for k, value in values.items():
            total = jnp.where(gap == k, value, total)
        return total.astype(jnp.bfloat16)

    first_x = banded({-2: 1.0, -1: -8.0, 1: 8.0, 2: -1.0})
    second_x = banded({-2: -1.0, -1: 16.0, 0: -90.0, 1: 16.0, 2: -1.0})
    for i in range(2):
        d_x[i * nx : (i + 1) * nx] = first_x
        l_x[i * nx : (i + 1) * nx] = second_x
    for i, k in enumerate((-2, -1, 1, 2)):
        move = banded({-k: 1.0})
        s_x[2 * i * nx : (2 * i + 1) * nx] = move
        s_x[(2 * i + 1) * nx : (2 * i + 2) * nx] = move

    pl.semaphore_wait(barrier, n - 1)

    def remote(src, dst, send, recv, to_y, to_z):
        return pltpu.make_async_remote_copy(
            src_ref=src, dst_ref=dst, send_sem=send, recv_sem=recv,
            device_id={"gy": to_y, "gz": to_z}, device_id_type=MESH,
        )

    up_y = lax.min(gy + 1, ny - 1)
    dn_y = lax.max(gy - 1, 0)
    up_z = lax.min(gz + 1, nz - 1)
    dn_z = lax.max(gz - 1, 0)
    y_up = [
        [
            remote(a.at[c, pl.ds(cy - 2, 2)], F.at[3 * i + c, 0:2, zin], y_send.at[6 * i + c], y_recv.at[6 * i + c], up_y, gz)
            for i, a in enumerate((om, ve))
        ]
        for c in range(3)
    ]
    y_dn = [
        [
            remote(a.at[c, pl.ds(0, 2)], F.at[3 * i + c, pl.ds(cy + 2, 2), zin], y_send.at[6 * i + 3 + c], y_recv.at[6 * i + 3 + c], dn_y, gz)
            for i, a in enumerate((om, ve))
        ]
        for c in range(3)
    ]
    for c in range(3):

        @pl.when(hi_y)
        def _(c=c):
            y_up[c][0].start()
            y_up[c][1].start()

        @pl.when(lo_y)
        def _(c=c):
            y_dn[c][0].start()
            y_dn[c][1].start()

    load_v.wait()

    load_o.wait()

    for side, row in ((0, cz - 2), (1, 0)):
        for c in range(6):
            zsend[side, c] = F[c, 2 : 2 + cy, 8 + row : 10 + row, :]
    z_copy = [
        remote(zsend.at[0], zrecv.at[0], z_send.at[0], z_recv.at[0], gy, up_z),
        remote(zsend.at[1], zrecv.at[1], z_send.at[1], z_recv.at[1], gy, dn_z),
    ]

    @pl.when(hi_z)
    def _():
        z_copy[0].start()

    @pl.when(lo_z)
    def _():
        z_copy[1].start()

    @pl.when(has)
    def _():
        win = pl.ds(base, WINDOW)
        cell = cells[:, win]
        frac = fracs[:, win]
        own = owner[win].reshape(1, WINDOW)

        def table(length, at, which):
            rows = lax.broadcasted_iota(jnp.int32, (length, WINDOW), 0)
            gap = rows + (at - cell[which : which + 1])
            return remesh_kernel(gap.astype(jnp.float32) - frac[which : which + 1])

        t_x = table(nx, 0, 0)
        high, low = split(t_x)
        tx_h[...] = high
        tx_l[...] = low
        high, low = split(t_x.T)
        tt_h[...] = high
        tt_l[...] = low
        ty[...] = table(cy, (gy - own // nz) * cy, 1)
        tz[...] = table(cz, (gz - own % nz) * cz, 2)
        acc[...] = jnp.zeros_like(acc)

        def layer(y, carry):
            block = F[3:6, y + 2, 8 : 8 + cz, :].reshape(3 * cz, nx)
            high, low = split(block)
            both = dot(high, tx_h[...]) + (dot(low, tx_h[...]) + dot(high, tx_l[...]))
            both = both.reshape(3, cz, WINDOW) * tz[...][None]
            acc[0:3, :] += jnp.sum(both, axis=1) * ty[pl.ds(y, 1), :]
            return carry

        lax.fori_loop(0, cy, layer, 0)
        slots[slot, 0:3, :] = acc[0:3, 0:LANES]
        slots[slot, 3:6, :] = acc[0:3, LANES:WINDOW]

        def send_peer(b, carry):
            to_y = rotor * span_blocks + b // vert_blocks
            to_z = vert_first + b % vert_blocks
            d = to_y * nz + to_z

            @pl.when(d != me)
            def _():
                remote(slots.at[slot], slots.at[slot], s_send.at[d], s_recv.at[slot], to_y, to_z).start()

            return carry

        lax.fori_loop(0, group, send_peer, 0)

    def send_rest(i, carry):
        d = (me + i) % n
        to_y, to_z = d // nz, d % nz
        peer = (
            (to_y // span_blocks == rotor) & (to_y < span_blocks * TURBINES)
            & (to_z >= vert_first) & (to_z < vert_first + vert_blocks)
        )

        @pl.when(has & jnp.logical_not(peer))
        def _():
            remote(slots.at[slot], slots.at[slot], s_send.at[d], s_recv.at[slot], to_y, to_z).start()

        return carry

    lax.fori_loop(1, n, send_rest, 0)

    def slot_wait(k):
        @pl.when(jnp.logical_not(has & (k == slot)))
        def _():
            remote(slots.at[k], slots.at[k], s_send.at[0], s_recv.at[k], gy, gz).wait_recv()

    @pl.when(has)
    def _():
        def take(b, carry):
            slot_wait(rotor * group + b)
            tile = slots[rotor * group + b]
            acc[0:3, 0:LANES] += tile[0:3]
            acc[0:3, LANES:WINDOW] += tile[3:6]
            return carry

        acc[...] = jnp.zeros_like(acc)
        lax.fori_loop(0, group, take, 0)
        win = pl.ds(base, WINDOW)
        vel = [acc[c : c + 1, :] for c in range(3)]
        forces = blade_forces(vel, chord[win].reshape(1, WINDOW), twist[win].reshape(1, WINDOW), angle[0], base, WINDOW)
        for c in range(3):
            srow[c : c + 1, :] = section_step * forces[c]

        def layer(y, carry):
            spread = jnp.concatenate([tz[...] * (ty[pl.ds(y, 1), :] * srow[c : c + 1, :]) for c in range(3)], axis=0)
            high, low = split(spread)
            total = dot(high, tt_h[...]) + (dot(low, tt_h[...]) + dot(high, tt_l[...]))
            smear[:, y] = total.reshape(3, cz, nx)
            return carry

        lax.fori_loop(0, cy, layer, 0)

    @pl.when(jnp.logical_not(has))
    def _():
        smear[...] = jnp.zeros_like(smear)

    @pl.when(lo_z)
    def _():
        z_copy[0].wait_recv()

    @pl.when(hi_z)
    def _():
        z_copy[1].wait_recv()

    for c in range(6):
        F[c, 2 : 2 + cy, 6:8, :] = zrecv[0, c]
        F[c, 2 : 2 + cy, 8 + cz : 10 + cz, :] = zrecv[1, c]

    ROWS = 8
    d1 = 1.0 / 12.0

    def section_layer(y, comps=(0, 1, 2)):
        def stencil(start, matrix):
            block = jnp.concatenate([F[start + c, y + 2, 8 : 8 + cz, :] for c in comps], axis=0)
            return dot(jnp.concatenate(split(block), axis=1), matrix[...])

        along = stencil(3, d_x)
        bent = stencil(0, l_x)
        taps = tap_weights(F[3, y + 2, 8 : 8 + cz, :])
        w = [F[c, y + 2, 8 : 8 + cz, :] for c in range(3)]
        kept, sides = [], []
        for i, c in enumerate(comps):
            def yv(a, k):
                return F[a, y + 2 + k, 8 : 8 + cz, :]

            def zv(a, k):
                return F[a, y + 2, 8 + k : 8 + k + cz, :]

            v = 3 + c
            rows = slice(i * cz, (i + 1) * cz)
            dy = 8.0 * (yv(v, 1) - yv(v, -1)) - (yv(v, 2) - yv(v, -2))
            dz = 8.0 * (zv(v, 1) - zv(v, -1)) - (zv(v, 2) - zv(v, -2))
            stretch = w[2] * along[rows] + w[1] * dz + w[0] * dy
            near = (yv(c, 1) + yv(c, -1)) + (zv(c, 1) + zv(c, -1))
            wide = (yv(c, 2) + yv(c, -2)) + (zv(c, 2) + zv(c, -2))
            lap = 16.0 * near - wide + bent[rows]
            value = w[c] + (section_step * d1) * (stretch + viscosity * lap) + smear[c, y]
            kept.append(taps[2] * value)
            pieces = []
            for k in (0, 1, 3, 4):
                pieces.extend(split(taps[k] * value))
            sides.append(jnp.concatenate(pieces, axis=1))
        total = dot(jnp.concatenate(sides, axis=0), s_x[...])
        for i, c in enumerate(comps):
            M[c, y + 2] = kept[i] + total[i * cz : (i + 1) * cz]

    def span_layer(y, comps=(0, 1, 2)):
        for z0 in range(0, cz, ROWS):
            totals = {}
            for k in range(-2, 3):
                weight = tap_weights(F[4, y + 2 - k, 8 + z0 : 8 + z0 + ROWS, :])[k + 2]
                for c in comps:
                    part = weight * M[c, y + 2 - k, z0 : z0 + ROWS, :]
                    totals[c] = totals[c] + part if c in totals else part
            for c in comps:
                N[c, y, z0 : z0 + ROWS, :] = totals[c]

    def over(first, last, body):
        def step(y, carry):
            body(y)
            return carry

        lax.fori_loop(first, last, step, 0)

    def over_edges(body):
        def step(i, carry):
            body(jnp.where(i < 2, i, cy - 4 + i))
            return carry

        lax.fori_loop(0, 4, step, 0)

    over(2, cy - 2, section_layer)

    v_up, v_dn = [], []
    for c in range(3):

        @pl.when(lo_y)
        def _(c=c):
            y_up[c][0].wait_recv()
            y_up[c][1].wait_recv()

        @pl.when(hi_y)
        def _(c=c):
            y_dn[c][0].wait_recv()
            y_dn[c][1].wait_recv()

        over_edges(functools.partial(section_layer, comps=(c,)))
        v_up.append(remote(M.at[c, pl.ds(cy, 2)], M.at[c, 0:2], v_send.at[c], v_recv.at[c], up_y, gz))
        v_dn.append(remote(M.at[c, 2:4], M.at[c, pl.ds(cy + 2, 2)], v_send.at[3 + c], v_recv.at[3 + c], dn_y, gz))

        @pl.when(hi_y)
        def _(c=c):
            v_up[c].start()

        @pl.when(lo_y)
        def _(c=c):
            v_dn[c].start()

    over(2, cy - 2, span_layer)
    stores = [
        pltpu.make_async_copy(N.at[:, part], moved.at[:, part], out_sem.at[i])
        for i, part in enumerate((pl.ds(2, cy - 4), pl.ds(0, 2), pl.ds(cy - 2, 2)))
    ]
    stores[0].start()
    w_copy = [[], []]

    def rims(number, first, length):
        for side, row in ((0, cz - 2), (1, 0)):
            for c in range(3):
                wsend[side, c, first : first + length] = N[c, first : first + length, row : row + 2, :]
            w_copy[side].append(remote(
                wsend.at[side, :, first : first + length], wrecv.at[side, 0:3, first : first + length],
                w_send.at[2 * number + side], w_recv.at[2 * number + side], gy, (up_z, dn_z)[side],
            ))

        @pl.when(hi_z)
        def _():
            w_copy[0][number].start()

        @pl.when(lo_z)
        def _():
            w_copy[1][number].start()

    rims(0, 2, cy - 4)

    count = sources.shape[1]
    sources[...] = jnp.zeros_like(sources)

    for t in range(TURBINES):
        first = (t // 2) * (2 * ROTOR) + (t % 2) * LANES

        def gather(b, carry, t=t, first=first):
            k = t * group + b

            @pl.when(jnp.logical_not(has & (rotor == t)))
            def _():
                slot_wait(k)

            tile = slots[k]
            sources[0:3, first : first + LANES] += tile[0:3]
            sources[0:3, first + LANES : first + WINDOW] += tile[3:6]
            return carry

        lax.fori_loop(0, group, gather, 0)
    forces = blade_forces(
        [sources[c : c + 1, :] for c in range(3)], chord[...].reshape(1, count), twist[...].reshape(1, count),
        angle[0], 0, count,
    )
    for c in range(3):
        sources[c : c + 1, :] = forces[c]

    for c in range(3):

        @pl.when(lo_y)
        def _(c=c):
            v_up[c].wait_recv()

        @pl.when(hi_y)
        def _(c=c):
            v_dn[c].wait_recv()

        over_edges(functools.partial(span_layer, comps=(c,)))

    stores[1].start()
    stores[2].start()
    rims(1, 0, 2)
    rims(2, cy - 2, 2)
    for side in range(2):
        wrecv[side, 3] = zrecv[side, 5]
    for i in range(3):

        @pl.when(lo_z)
        def _(i=i):
            w_copy[0][i].wait_recv()

        @pl.when(hi_z)
        def _(i=i):
            w_copy[1][i].wait_recv()

    rim_store = pltpu.make_async_copy(wrecv, rim, rim_sem)
    rim_store.start()

    @pl.when(hi_y)
    def _():
        for c in range(3):
            y_up[c][0].wait_send()
            y_up[c][1].wait_send()
            v_up[c].wait_send()

    @pl.when(lo_y)
    def _():
        for c in range(3):
            y_dn[c][0].wait_send()
            y_dn[c][1].wait_send()
            v_dn[c].wait_send()

    @pl.when(hi_z)
    def _():
        z_copy[0].wait_send()
        for i in range(3):
            w_copy[0][i].wait_send()

    @pl.when(lo_z)
    def _():
        z_copy[1].wait_send()
        for i in range(3):
            w_copy[1][i].wait_send()

    def sent(i, carry):
        d = (me + i) % n

        @pl.when(has)
        def _():
            remote(slots.at[slot], slots.at[slot], s_send.at[d], s_recv.at[0], gy, gz).wait_send()

        return carry

    lax.fori_loop(1, n, sent, 0)
    for store in stores:
        store.wait()
    rim_store.wait()


def vertical_kernel(moved, speed, rim, given, out, sources, G):
    _, rows, cz, nx = moved.shape
    for c in range(4):
        G[c, :, 8 : 8 + cz, :] = moved[c] if c < 3 else speed[0]
        G[c, :, 6:8, :] = rim[0, c]
        G[c, :, 8 + cz : 10 + cz, :] = rim[1, c]
    sources[...] = given[...]

    def layer(y, carry):
        for z0 in range(0, cz, 8):
            totals = [None] * 3
            for k in range(-2, 3):
                at = 8 + z0 - k
                weight = tap_weights(G[3, y, at : at + 8, :])[k + 2]
                for c in range(3):
                    part = weight * G[c, y, at : at + 8, :]
                    totals[c] = part if totals[c] is None else totals[c] + part
            for c in range(3):
                out[c, y, z0 : z0 + 8, :] = totals[c]
        return carry

    lax.fori_loop(0, rows, layer, 0)


def on_device(ny, nz, omega, velocity, point_owner, point_cells, point_frac, chord, twist, angle_step):
    _, cy, cz, nx = omega.shape
    points = point_owner.shape[0]
    n = ny * nz
    nslots = TURBINES * (ny // TURBINES) * max(nz // 2, 1)
    f32, bf16 = jnp.float32, jnp.bfloat16
    vmem = pl.BlockSpec(memory_space=pltpu.VMEM)
    hbm = pl.BlockSpec(memory_space=pl.ANY)
    given = pl.BlockSpec(memory_space=pltpu.HBM)
    dma = pltpu.SemaphoreType.DMA
    moved, rim, sources = pl.pallas_call(
        functools.partial(kernel, ny, nz),
        out_shape=(
            jax.ShapeDtypeStruct(omega.shape, f32),
            jax.ShapeDtypeStruct((2, 4, cy, 2, nx), f32),
            jax.ShapeDtypeStruct((3, points), f32),
        ),
        in_specs=[given, given, vmem, vmem, vmem, vmem, vmem, pl.BlockSpec(memory_space=pltpu.SMEM)],
        out_specs=(hbm, hbm, vmem),
        scratch_shapes=[
            pltpu.VMEM((6, cy + 4, cz + 16, nx), f32),
            pltpu.VMEM((3, cy + 4, cz, nx), f32),
            pltpu.VMEM((3, cy, cz, nx), f32),
            pltpu.VMEM((3, cy, cz, nx), f32),
            pltpu.VMEM((2 * nx, nx), bf16),
            pltpu.VMEM((2 * nx, nx), bf16),
            pltpu.VMEM((8 * nx, nx), bf16),
            pltpu.VMEM((nslots, 8, LANES), f32),
            pltpu.VMEM((8, WINDOW), f32),
            pltpu.VMEM((nx, WINDOW), bf16),
            pltpu.VMEM((nx, WINDOW), bf16),
            pltpu.VMEM((cy, WINDOW), f32),
            pltpu.VMEM((cz, WINDOW), f32),
            pltpu.VMEM((WINDOW, nx), bf16),
            pltpu.VMEM((WINDOW, nx), bf16),
            pltpu.VMEM((8, WINDOW), f32),
            pltpu.VMEM((2, 6, cy, 2, nx), f32),
            pltpu.VMEM((2, 6, cy, 2, nx), f32),
            pltpu.VMEM((2, 3, cy, 2, nx), f32),
            pltpu.VMEM((2, 4, cy, 2, nx), f32),
            dma((2,)),
            dma((3,)),
            dma,
            dma((12,)),
            dma((12,)),
            dma((2,)),
            dma((2,)),
            dma((6,)),
            dma((6,)),
            dma((6,)),
            dma((6,)),
            dma((n,)),
            dma((nslots,)),
        ],
        compiler_params=pltpu.CompilerParams(
            collective_id=0, has_side_effects=True, vmem_limit_bytes=60 * 1024 * 1024
        ),
        name="wake_step",
    )(
        omega,
        velocity,
        point_cells,
        point_frac,
        point_owner,
        chord,
        twist,
        angle_step,
    )
    rows = 4 if cy % 4 == 0 else cy
    every = pl.BlockSpec((3, points), lambda i: (0, 0))
    field = pl.BlockSpec((3, rows, cz, nx), lambda i: (0, i, 0, 0))
    return pl.pallas_call(
        vertical_kernel,
        out_shape=(
            jax.ShapeDtypeStruct(omega.shape, f32),
            jax.ShapeDtypeStruct((3, points), f32),
        ),
        grid=(cy // rows,),
        in_specs=[
            field,
            pl.BlockSpec((1, rows, cz, nx), lambda i: (2, i, 0, 0)),
            pl.BlockSpec((2, 4, rows, 2, nx), lambda i: (0, 0, i, 0, 0)),
            every,
        ],
        out_specs=(field, every),
        scratch_shapes=[pltpu.VMEM((4, rows, cz + 16, nx), f32)],
        compiler_params=pltpu.CompilerParams(vmem_limit_bytes=16 * 1024 * 1024),
        name="wake_vertical",
    )(moved, velocity, rim, sources)


def solution(mesh):
    in_specs = (P(None, "gy", "gz", None), P(None, "gy", "gz", None), P(), P(), P(), P(), P(), P())
    out_specs = (P(None, "gy", "gz", None), P())
    return jax.shard_map(
        functools.partial(on_device, mesh.shape["gy"], mesh.shape["gz"]),
        mesh=mesh, in_specs=in_specs, out_specs=out_specs, check_vma=False,
    )
```

time: 164 us -> 39.8 us (0.24)
  blocking collectives: 42.3 us -> 0 us
  Pallas kernels: 0 us -> 35.3 us
  other arithmetic: 33.1 us -> 0 us
  starting transfers between devices: 32 us -> 0 us
  matrix products: 25.8 us -> 0 us
  local copies, waits for them, and re-layouts: 22.7 us -> 3.03 us
  waiting for transfers between devices: 5.01 us -> 0 us
    psum x1 -> x0, blocking collectives: 42.3 us -> none  [on_device(): point_velocity = lax.psum(partial_velocity, ('gy', 'gz'))]
    pallas_call x0 -> x2, Pallas kernels: none -> 35.3 us  [the longest x1 32.3 us: on_device(): pl.pallas_call(functools.partial(kernel, ny, nz), out_shape=(jax.ShapeDty...]
    ppermute x12 -> x0, starting transfers between devices: 32 us -> none  [the longest x6 21.6 us: with_halo(): after = lax.ppermute(initial, axis, down)]
    dot_general x4 -> x0, matrix products: 25.8 us -> none  [the longest x1 20.4 us: on_device(): jnp.dot(spread.reshape(-1, spread.shape[3]), table_x.T, precision=highest...]
    add x6 -> x0, other arithmetic: 9.89 us -> none  [the longest x3 9.8 us: remesh_padded(): total = total + remesh_kernel(offset - moved)[None] * part]
    select_n x5 -> x0, other arithmetic: 7.59 us -> none  [the longest x4 7.58 us: remesh_kernel(): return jnp.where(mag < 1.0, inner, jnp.where(mag < 2.0, outer, 0.0))]
    gather x6 -> x0, local copies, waits for them, and re-layouts: 6.1 us -> none  [the longest x2 1.82 us: on_device(): local_sources = sources[:, picked]]
    concatenate x2 -> x0, other arithmetic: 5.26 us -> none  [with_halo(): x = jnp.concatenate([before, x, after], axis=dim)]
  transfers between devices with their start and end apart: 12 -> 0, of which waited for: 2 -> 0; matrix products, arithmetic and copies ran while one was open for 27% -> 0% of each run, Pallas kernels for 0% -> 0%
where the time goes in v1:
time: 39.8 us; the launch traced here: 39.6 us
  Pallas kernels  35.3 us (89%)
  local copies, waits for them, and re-layouts  3.03 us (8%)
  between operations  1.31 us (3%)
    pallas_call x1, Pallas kernels, on_device(): pl.pallas_call(functools.partial(kernel, ny, nz), out_shape=(jax.ShapeDty...  32.3 us
    unnamed x8, local copies, waits for them, and re-layouts  3.03 us
    pallas_call x1, Pallas kernels, on_device(): pl.pallas_call(vertical_kernel, out_shape=(jax.ShapeDtypeStruct(omega.sha...  2.95 us

profile of v1, /device:TPU:6, one launch (start us, length us, event | category | flops | bytes accessed | tf_op | source)
XLA Modules:
  0.0 39.6 jit_solution(1982103893152635100)
XLA Ops:
  1.3 0.0 copy-start
  1.3 32.3 %wake_step.1 = (f32[3,16,64,128]{3,2,1,0:T(8,128)}, f32[2,4,16,2,128]{4,3,2,1,0:T(2,128)}, f32[3,1152]{1,0:T(4,128)}) custom-call(f32[3,16,64,128]{3,2,1,0:T(8,128)} %om.1, f32[3,16,64,128]{3,2,1,0:T(8,128)} %speed.1, s32[3,1152]{1,0:T(4,128)} %cells.1, f32[3,1152]{1,0:T(4,128)} %fracs.1, s32[1152]{0:T(1024)} %owner.1, f32[1152]{0:T(1024)} %chord.1, ...), custom_call_target="tpu_custom_call" | custom-call | tf_op jit(solution)/shard_map/wake_step/pallas_call | solution.py:577
  33.6 0.0 copy-done
  33.6 0.0 copy-start.1
  33.6 1.4 %copy-done.1 = f32[3,16,64,128]{3,2,1,0:T(8,128)S(1)} copy-done((f32[3,16,64,128]{3,2,1,0:T(8,128)S(1)}, f32[3,16,64,128]{3,2,1,0:T(8,128)}, u32[]{:S(2)}) %copy-start.1) | copy-done | bytes 1572888
  35.0 0.0 copy-start.2
  35.0 0.9 %copy-done.2 = f32[2,4,16,2,128]{4,3,2,1,0:T(2,128)S(1)} copy-done((f32[2,4,16,2,128]{4,3,2,1,0:T(2,128)S(1)}, f32[2,4,16,2,128]{4,3,2,1,0:T(2,128)}, u32[]{:S(2)}) %copy-start.2) | copy-done | bytes 131096
  35.9 0.0 copy-start.3
  35.9 0.7 %copy-done.3 = f32[3,1152]{1,0:T(4,128)S(1)} copy-done((f32[3,1152]{1,0:T(4,128)S(1)}, f32[3,1152]{1,0:T(4,128)}, u32[]{:S(2)}) %copy-start.3) | copy-done | bytes 13848
  36.7 2.9 %wake_vertical.1 = (f32[3,16,64,128]{3,2,1,0:T(8,128)}, f32[3,1152]{1,0:T(4,128)}) custom-call(f32[3,16,64,128]{3,2,1,0:T(8,128)S(1)} %copy-done.1, f32[3,16,64,128]{3,2,1,0:T(8,128)S(1)} %copy-done, f32[2,4,16,2,128]{4,3,2,1,0:T(2,128)S(1)} %copy-done.2, f32[3,1152]{1,0:T(4,128)S(1)} %copy-done.3), custom_call_target="tpu_custom_call" | custom-call | tf_op jit(solution)/shard_map/wake_vertical/pallas_call | solution.py:638
Async XLA Ops:
  1.3 32.3 %copy-start = (f32[3,16,64,128]{3,2,1,0:T(8,128)S(1)}, f32[3,16,64,128]{3,2,1,0:T(8,128)}, u32[]{:S(2)}) copy-start(f32[3,16,64,128]{3,2,1,0:T(8,128)} %speed.1) | copy-start | bytes 4718596
  33.6 1.4 %copy-start.1 = (f32[3,16,64,128]{3,2,1,0:T(8,128)S(1)}, f32[3,16,64,128]{3,2,1,0:T(8,128)}, u32[]{:S(2)}) copy-start(f32[3,16,64,128]{3,2,1,0:T(8,128)} %get-tuple-element.5.moved) | copy-start | bytes 4718596
  35.0 0.9 %copy-start.2 = (f32[2,4,16,2,128]{4,3,2,1,0:T(2,128)S(1)}, f32[2,4,16,2,128]{4,3,2,1,0:T(2,128)}, u32[]{:S(2)}) copy-start(f32[2,4,16,2,128]{4,3,2,1,0:T(2,128)} %get-tuple-element.6.rim) | copy-start | bytes 393220
  35.9 0.7 %copy-start.3 = (f32[3,1152]{1,0:T(4,128)S(1)}, f32[3,1152]{1,0:T(4,128)}, u32[]{:S(2)}) copy-start(f32[3,1152]{1,0:T(4,128)} %get-tuple-element.7.given) | copy-start | bytes 41476
